TPU v7x, 32 devices: a whole 2x2x4 slice. The times are simulated.
32 devices in a mesh: gx: 16 (over z, y, x), gy: 2 (over core).
Axes of the slice: x: 2, y: 2, z: 4, core: 2. Of those that a mesh axis runs over, the one named last changes fastest.
Arguments:
- residual: bfloat16 [16, 2, 2048, 384], P('gx', 'gy'), may hold values from -6 to 6
- local_inverse: bfloat16 [16, 2, 2048, 2048], P('gx', 'gy'), may hold values from -0.125 to 0.125
- primal_basis: bfloat16 [16, 2, 96, 2048], P('gx', 'gy'), may hold values from -0.125 to 0.125
- row_stiffness: bfloat16 [16, 2, 2048], P('gx', 'gy'), may hold values from 0.099609375 to 10
- face_sizes: int32 [16, 2, 4], P('gx', 'gy'), may hold values from 0 to 512, as said below
- primal_slots: int32 [16, 2, 96], P('gx', 'gy'), may hold values from 0 to 287
- block_inverse: float32 [16, 2, 32, 64], P('gx', 'gy'), may hold values from -1 to 3
- level_basis: float32 [16, 2, 32, 64], P('gx', 'gy'), may hold values from -0.15625 to 0.15625
- top_inverse: float32 [64, 64], replicated, may hold values from -1 to 3
Outputs:
- preconditioned: bfloat16 [16, 2, 2048, 384], P('gx', 'gy')
Inputs may be any that keep to these rules, and one draw needn't show every extreme that they name: face_sizes[x, y, f] is equal on the two sides of a shared face, 0 on faces at the grid's edge, at least 128 elsewhere; the value 512 is reached.
All inputs are finite; a program needn't handle non-finite values.
Results may differ from a plain program's by a relative error of at most 0.008.
Values may be sent and summed in bfloat16 or wider, within the bound.
No kernel may reach another device: no remote copies, remote signals or barrier semaphores. Data moves between devices by JAX's collectives and lax.ppermute only.
A program may use at most 64 MiB of HBM per device.

v0:
```python
import jax
import jax.numpy as jnp
from jax import lax
from jax.sharding import PartitionSpec as P


def passed_along(block, axis, distance):
    devices = range(lax.axis_size(axis))
    route = [(i - distance, i) for i in devices if i - distance in devices]
    return lax.ppermute(block, axis, route)


def extended(block, sides, width):
    for axis, dim in sides:
        count = lax.axis_size(axis)
        forward = [(i, i + 1) for i in range(count - 1)]
        backward = [(target, source) for source, target in forward]
        low = lax.ppermute(
            lax.slice_in_dim(block, block.shape[dim] - width, None, axis=dim), axis, forward
        )
        high = lax.ppermute(lax.slice_in_dim(block, 0, width, axis=dim), axis, backward)
        block = jnp.concatenate([low, block, high], axis=dim)
    return block


def coarse_lift(phi_block, values, stiffness_block):
    coarse_rows = jnp.einsum("pw,pr->wr", phi_block, values, precision=lax.Precision.HIGHEST)
    return stiffness_block[:, None] * coarse_rows


def local(
    residual,
    local_inverse,
    primal_basis,
    row_stiffness,
    face_sizes,
    primal_slots,
    block_inverse,
    level_basis,
    top_inverse,
):
    highest = lax.Precision.HIGHEST
    own_rows = residual[0, 0]
    row_count = own_rows.shape[0]
    face_rows = row_count // 4
    coarse_count = block_inverse.shape[2]
    counts = face_sizes[0, 0]
    position = jnp.arange(row_count, dtype=jnp.int32)
    face_of_row = position // face_rows
    picked = jnp.where(
        face_of_row[:, None] == jnp.arange(4, dtype=jnp.int32)[None, :], counts[None, :], 0
    )
    live_rows = position % face_rows < jnp.sum(picked, axis=1)
    masked = jnp.where(live_rows[:, None], own_rows, jnp.zeros((), jnp.bfloat16))
    local_part = jnp.dot(local_inverse[0, 0], masked, preferred_element_type=jnp.float32)
    primal_phi = primal_basis[0, 0]
    partial_value = jnp.dot(primal_phi, masked, preferred_element_type=jnp.float32)
    selector = (
        primal_slots[0, 0][:, None] == jnp.arange(9 * coarse_count, dtype=jnp.int32)[None, :]
    ).astype(jnp.float32)
    spread = jnp.einsum("ps,pr->sr", selector, partial_value, precision=highest).reshape(
        3, 3, coarse_count, -1
    )
    from_below_y = passed_along(spread[:, 2], "gy", 1)
    from_above_y = passed_along(spread[:, 0], "gy", -1)
    along_x = spread[:, 1] + from_below_y + from_above_y
    from_below_x = passed_along(along_x[2], "gx", 1)
    from_above_x = passed_along(along_x[0], "gx", -1)
    assembled = along_x[1] + from_below_x + from_above_x
    level_phi = level_basis[0, 0]
    top_rhs = lax.psum(
        jnp.einsum("cl,cr->lr", level_phi, assembled, precision=highest), ("gx", "gy")
    )
    top_value = jnp.dot(top_inverse, top_rhs, precision=highest)
    block_rhs = lax.all_gather(assembled, "gy", axis=0, tiled=True)
    coarse = jnp.dot(block_inverse[0, 0], block_rhs, precision=highest) + jnp.dot(
        level_phi, top_value, precision=highest
    )
    beside_all = extended(coarse[None, None], (("gx", 0), ("gy", 1)), 1)
    primal_values = jnp.dot(selector, beside_all.reshape(9 * coarse_count, -1), precision=highest)
    stiffness = row_stiffness[0, 0]
    stiffness_f = stiffness.astype(jnp.float32)
    phi_f = primal_phi.astype(jnp.float32)
    local_weighted = jnp.where(live_rows[:, None], stiffness_f[:, None] * local_part, 0.0)
    own_total = local_weighted + coarse_lift(phi_f, primal_values, stiffness_f)
    sent = jnp.where(live_rows[:, None], own_total, 0.0).astype(jnp.bfloat16)

    def face_parts(values):
        return [values[face_id * face_rows : (face_id + 1) * face_rows] for face_id in range(4)]

    stiff_faces = face_parts(stiffness)
    sent_faces = face_parts(sent)
    recv_low_x = passed_along((sent_faces[1], stiff_faces[1]), "gx", 1)
    recv_high_x = passed_along((sent_faces[0], stiff_faces[0]), "gx", -1)
    recv_low_y = passed_along((sent_faces[3], stiff_faces[3]), "gy", 1)
    recv_high_y = passed_along((sent_faces[2], stiff_faces[2]), "gy", -1)
    received = [recv_low_x, recv_high_x, recv_low_y, recv_high_y]
    other_sent = jnp.concatenate([item[0] for item in received], axis=0)
    other_stiffness = jnp.concatenate([item[1] for item in received], axis=0)
    summed = sent.astype(jnp.float32) + other_sent.astype(jnp.float32)
    divisor = stiffness_f + other_stiffness.astype(jnp.float32)
    result = jnp.where(live_rows[:, None], summed / divisor[:, None], 0.0).astype(jnp.bfloat16)
    return result[None, None]


def solution(mesh):
    in_specs = (
        P("gx", "gy", None, None),
        P("gx", "gy", None, None),
        P("gx", "gy", None, None),
        P("gx", "gy", None),
        P("gx", "gy", None),
        P("gx", "gy", None),
        P("gx", "gy", None, None),
        P("gx", "gy", None, None),
        P(),
    )
    out_specs = P("gx", "gy", None, None)
    return jax.shard_map(local, mesh=mesh, in_specs=in_specs, out_specs=out_specs, check_vma=False)
```

profile of v0, /device:TPU:0, one launch (start us, length us, event | category | flops | bytes accessed | tf_op | source)
XLA Modules:
  0.0 225.4 jit_solution(7290555290257131025)
XLA Ops:
  7.6 2.4 %fusion.7 = f32[384,96]{1,0:T(8,128)S(1)} fusion(bf16[1,1,2048,384]{3,2,1,0:T(8,128)(2,1)} %param.9, pred[2048]{0:T(1024)(128)(4,1)S(1)} %fusion.29, bf16[1,1,96,2048]{3,2,1,0:T(8,128)(2,1)S(1)} %copy-done), kind=kOutput, calls=%fused_computation.5 | convolution fusion | flops 151781376 | bytes 2115584 | tf_op jit(solution)/shard_map/dot_general | solution.py:57
  10.5 2.4 %collective-permute-start = (f32[3,32,384]{2,1,0:T(8,128)S(1)}, f32[3,32,384]{2,1,0:T(8,128)S(1)}, u32[]{:S(2)}, u32[]{:S(2)}) collective-permute-start(f32[3,32,384]{2,1,0:T(8,128)S(1)} %get-tuple-element.13), channel_id=1, source_target_pairs={{0,1},{2,3},{4,5},{6,7},{8,9},{10,11},{12,13},{14,15},{16,17},{18,... | collective-permute-start | bytes 442376 | tf_op jit(solution)/shard_map/ppermute | solution.py:10
  12.9 1.3 collective-permute-start.1
  14.2 2.0 collective-permute-done.1
  16.2 4.2 %collective-permute-start.2 = (f32[32,384]{1,0:T(8,128)S(1)}, f32[32,384]{1,0:T(8,128)S(1)}, u32[]{:S(2)}, u32[]{:S(2)}) collective-permute-start(f32[32,384]{1,0:T(8,128)S(1)} %get-tuple-element.15), channel_id=1, source_target_pairs={{0,2},{2,4},{4,6},{6,8},{8,10},{10,12},{12,14},{14,16},{16,18},{18... | collective-permute-start | bytes 147464 | tf_op jit(solution)/shard_map/ppermute | solution.py:10
  20.4 1.3 collective-permute-start.3
  22.1 4.3 %collective-permute-done.3 = f32[32,384]{1,0:T(8,128)S(1)} collective-permute-done((f32[32,384]{1,0:T(8,128)S(1)}, f32[32,384]{1,0:T(8,128)S(1)}, u32[]{:S(2)}, u32[]{:S(2)}) %collective-permute-start.3) | collective-permute-done | bytes 49184 | tf_op jit(solution)/shard_map/ppermute | solution.py:10
  26.4 1.2 convolution_bitcast_fusion
  27.6 1.9 all_gather.3
  29.5 125.0 %all-reduce.2.cloned.1.call-done = f32[64,384]{0,1:T(8,128)} async-done(((f32[64,384]{0,1:T(8,128)}), f32[64,384]{0,1:T(8,128)}) %all-reduce.2.cloned.1.call-update) | async-done | bytes 98320 | tf_op jit(solution)/shard_map/psum | solution.py:71
  154.5 1.2 fusion.38
  156.3 3.4 %collective-permute-start.4 = (f32[1,1,32,384]{3,2,1,0:T(8,128)S(1)}, f32[1,1,32,384]{3,2,1,0:T(8,128)S(1)}, u32[]{:S(2)}, u32[]{:S(2)}) collective-permute-start(f32[1,1,32,384]{3,2,1,0:T(8,128)S(1)} %fusion.11), channel_id=1, source_target_pairs={{0,2},{2,4},{4,6},{6,8},{8,10},{10,12},{12,14},{14,16},{16,18},{18... | collective-permute-start | bytes 147464 | tf_op jit(solution)/shard_map/ppermute | solution.py:18
  159.7 1.3 collective-permute-start.5
  161.4 4.3 %collective-permute-done.5 = f32[1,1,32,384]{3,2,1,0:T(8,128)S(1)} collective-permute-done((f32[1,1,32,384]{3,2,1,0:T(8,128)S(1)}, f32[1,1,32,384]{3,2,1,0:T(8,128)S(1)}, u32[]{:S(2)}, u32[]{:S(2)}) %collective-permute-start.5) | collective-permute-done | bytes 49184 | tf_op jit(solution)/shard_map/ppermute | solution.py:21
  165.7 1.3 collective-permute-start.6
  167.0 1.3 collective-permute-start.7
  168.3 1.9 collective-permute-done.7
  170.7 1.4 fusion.12
  172.1 7.5 %fusion.4 = bf16[2048,384]{0,1:T(8,128)(2,1)S(1)} fusion(f32[384,2048]{1,0:T(8,128)S(1)} %fusion.12, bf16[1,1,2048,2048]{3,2,1,0:T(8,128)(2,1)} %param.10, f32[2048]{0:T(1024)S(1)} %bitcast.75, pred[2048]{0:T(1024)(128)(4,1)S(1)} %fusion.29, bf16[1,1,2048,384]{3,2,1,0:T(8,128)(2,1)S(1)} %copy-done.6), kind=kOutput, calls=%fused_computation.4 | convolution fusion | flops 3226730496 | bytes 14690304 | tf_op jit(solution)/shard_map/dot_general | solution.py:55
  179.8 2.1 collective-permute-start.10
  181.8 1.3 collective-permute-start.11
  183.1 4.3 %collective-permute-start.8 = (bf16[512,384]{0,1:T(8,128)(2,1)S(1)}, bf16[512,384]{0,1:T(8,128)(2,1)S(1)}, u32[]{:S(2)}, u32[]{:S(2)}) collective-permute-start(bf16[512,384]{0,1:T(8,128)(2,1)S(1)} %get-tuple-element.9), channel_id=1, source_target_pairs={{0,2},{2,4},{4,6},{6,8},{8,10},{10,12},{12,14},{14,16},{16,18},{18... | collective-permute-start | bytes 1179656 | tf_op jit(solution)/shard_map/ppermute | solution.py:10
  187.4 1.3 collective-permute-start.9
  188.8 4.5 %collective-permute-start.12 = (bf16[512]{0:T(512)(128)(2,1)S(1)}, bf16[512]{0:T(512)(128)(2,1)S(1)}, u32[]{:S(2)}, u32[]{:S(2)}) collective-permute-start(bf16[512]{0:T(512)(128)(2,1)S(1)} %get-tuple-element.5), channel_id=1, source_target_pairs={{0,2},{2,4},{4,6},{6,8},{8,10},{10,12},{12,14},{14,16},{16,18},{18... | collective-permute-start | bytes 3080 | tf_op jit(solution)/shard_map/ppermute | solution.py:10
  193.3 11.8 %collective-permute-done.12 = bf16[512]{0:T(512)(128)(2,1)S(1)} collective-permute-done((bf16[512]{0:T(512)(128)(2,1)S(1)}, bf16[512]{0:T(512)(128)(2,1)S(1)}, u32[]{:S(2)}, u32[]{:S(2)}) %collective-permute-start.12) | collective-permute-done | bytes 1056 | tf_op jit(solution)/shard_map/ppermute | solution.py:10
  205.2 1.3 collective-permute-start.13
  206.5 4.7 %collective-permute-done.13 = bf16[512]{0:T(512)(128)(2,1)S(1)} collective-permute-done((bf16[512]{0:T(512)(128)(2,1)S(1)}, bf16[512]{0:T(512)(128)(2,1)S(1)}, u32[]{:S(2)}, u32[]{:S(2)}) %collective-permute-start.13) | collective-permute-done | bytes 1056 | tf_op jit(solution)/shard_map/ppermute | solution.py:10
  211.1 1.3 collective-permute-start.14
  212.4 0.8 collective-permute-done.14
  213.2 1.3 collective-permute-start.15
  214.5 1.8 collective-permute-done.15
  217.0 1.6 copy.15
  (42 shorter events, 4.2 us)
Async XLA Ops:
  6.5 1.0 copy-start
  6.5 3.4 %copy-start.5 = (s32[1,1,96]{2,1,0:T(1,128)S(1)}, s32[1,1,96]{2,1,0:T(1,128)}, u32[]{:S(2)}) copy-start(s32[1,1,96]{2,1,0:T(1,128)} %param.14) | copy-start | bytes 1156
  6.5 19.9 %copy-start.1 = (f32[1,1,32,64]{3,2,1,0:T(8,128)S(1)}, f32[1,1,32,64]{3,2,1,0:T(8,128)}, u32[]{:S(2)}) copy-start(f32[1,1,32,64]{3,2,1,0:T(8,128)} %param.16) | copy-start | bytes 24580
  6.5 147.9 %all-reduce.2.cloned.1.call-start = ((), (), s32[]{:S(2)}) async-start(), calls=%async_computation | async-start | bytes 393216 | tf_op jit(solution)/shard_map/psum | solution.py:71
  7.5 146.9 %copy-start.3 = (f32[64,64]{1,0:T(8,128)S(1)}, f32[64,64]{1,0:T(8,128)}, u32[]{:S(2)}) copy-start(f32[64,64]{1,0:T(8,128)} %param.17) | copy-start | bytes 49156
  7.5 148.5 %copy-start.4 = (f32[1,1,32,64]{3,2,1,0:T(8,128)S(1)}, f32[1,1,32,64]{3,2,1,0:T(8,128)}, u32[]{:S(2)}) copy-start(f32[1,1,32,64]{3,2,1,0:T(8,128)} %param.15) | copy-start | bytes 24580
  7.6 160.7 %copy-start.2 = (bf16[1,1,2048]{2,1,0:T(2,128)(2,1)S(1)}, bf16[1,1,2048]{2,1,0:T(2,128)(2,1)}, u32[]{:S(2)}) copy-start(bf16[1,1,2048]{2,1,0:T(2,128)(2,1)} %param.12) | copy-start | bytes 12292
  10.5 3.7 %collective-permute-start = (f32[3,32,384]{2,1,0:T(8,128)S(1)}, f32[3,32,384]{2,1,0:T(8,128)S(1)}, u32[]{:S(2)}, u32[]{:S(2)}) collective-permute-start(f32[3,32,384]{2,1,0:T(8,128)S(1)} %get-tuple-element.13), channel_id=1, source_target_pairs={{0,1},{2,3},{4,5},{6,7},{8,9},{10,11},{12,13},{14,15},{16,17},{18,... | collective-permute-start | bytes 442376 | tf_op jit(solution)/shard_map/ppermute | solution.py:10
  12.9 3.3 %collective-permute-start.1 = (f32[3,32,384]{2,1,0:T(8,128)S(1)}, f32[3,32,384]{2,1,0:T(8,128)S(1)}, u32[]{:S(2)}, u32[]{:S(2)}) collective-permute-start(f32[3,32,384]{2,1,0:T(8,128)S(1)} %get-tuple-element.14), channel_id=1, source_target_pairs={{1,0},{3,2},{5,4},{7,6},{9,8},{11,10},{13,12},{15,14},{17,16},{19,... | collective-permute-start | bytes 442376 | tf_op jit(solution)/shard_map/ppermute | solution.py:10
  16.2 6.0 %collective-permute-start.2 = (f32[32,384]{1,0:T(8,128)S(1)}, f32[32,384]{1,0:T(8,128)S(1)}, u32[]{:S(2)}, u32[]{:S(2)}) collective-permute-start(f32[32,384]{1,0:T(8,128)S(1)} %get-tuple-element.15), channel_id=1, source_target_pairs={{0,2},{2,4},{4,6},{6,8},{8,10},{10,12},{12,14},{14,16},{16,18},{18... | collective-permute-start | bytes 147464 | tf_op jit(solution)/shard_map/ppermute | solution.py:10
  20.4 6.0 %collective-permute-start.3 = (f32[32,384]{1,0:T(8,128)S(1)}, f32[32,384]{1,0:T(8,128)S(1)}, u32[]{:S(2)}, u32[]{:S(2)}) collective-permute-start(f32[32,384]{1,0:T(8,128)S(1)} %get-tuple-element.16), channel_id=1, source_target_pairs={{2,0},{4,2},{6,4},{8,6},{10,8},{12,10},{14,12},{16,14},{18,16},{20... | collective-permute-start | bytes 147464 | tf_op jit(solution)/shard_map/ppermute | solution.py:10
  29.5 142.6 %copy-start.6 = (bf16[1,1,2048,384]{3,2,1,0:T(8,128)(2,1)S(1)}, bf16[1,1,2048,384]{3,2,1,0:T(8,128)(2,1)}, u32[]{:S(2)}) copy-start(bf16[1,1,2048,384]{3,2,1,0:T(8,128)(2,1)} %param.9) | copy-start | bytes 4718596
  156.3 5.1 %collective-permute-start.4 = (f32[1,1,32,384]{3,2,1,0:T(8,128)S(1)}, f32[1,1,32,384]{3,2,1,0:T(8,128)S(1)}, u32[]{:S(2)}, u32[]{:S(2)}) collective-permute-start(f32[1,1,32,384]{3,2,1,0:T(8,128)S(1)} %fusion.11), channel_id=1, source_target_pairs={{0,2},{2,4},{4,6},{6,8},{8,10},{10,12},{12,14},{14,16},{16,18},{18... | collective-permute-start | bytes 147464 | tf_op jit(solution)/shard_map/ppermute | solution.py:18
  159.7 6.0 %collective-permute-start.5 = (f32[1,1,32,384]{3,2,1,0:T(8,128)S(1)}, f32[1,1,32,384]{3,2,1,0:T(8,128)S(1)}, u32[]{:S(2)}, u32[]{:S(2)}) collective-permute-start(f32[1,1,32,384]{3,2,1,0:T(8,128)S(1)} %fusion.11), channel_id=1, source_target_pairs={{2,0},{4,2},{6,4},{8,6},{10,8},{12,10},{14,12},{16,14},{18,16},{20... | collective-permute-start | bytes 147464 | tf_op jit(solution)/shard_map/ppermute | solution.py:21
  165.7 2.6 %collective-permute-start.6 = (f32[3,1,32,384]{3,2,1,0:T(8,128)S(1)}, f32[3,1,32,384]{3,2,1,0:T(8,128)S(1)}, u32[]{:S(2)}, u32[]{:S(2)}) collective-permute-start(f32[3,1,32,384]{3,2,1,0:T(8,128)S(1)} %pad_maximum_fusion.1), channel_id=1, source_target_pairs={{0,1},{2,3},{4,5},{6,7},{8,9},{10,11},{12,13},{14,15},{16,17},{18,... | collective-permute-start | bytes 442376 | tf_op jit(solution)/shard_map/ppermute | solution.py:18
  167.0 3.3 %collective-permute-start.7 = (f32[3,1,32,384]{3,2,1,0:T(8,128)S(1)}, f32[3,1,32,384]{3,2,1,0:T(8,128)S(1)}, u32[]{:S(2)}, u32[]{:S(2)}) collective-permute-start(f32[3,1,32,384]{3,2,1,0:T(8,128)S(1)} %pad_maximum_fusion.1), channel_id=1, source_target_pairs={{1,0},{3,2},{5,4},{7,6},{9,8},{11,10},{13,12},{15,14},{17,16},{19,... | collective-permute-start | bytes 442376 | tf_op jit(solution)/shard_map/ppermute | solution.py:21
  179.8 36.5 %collective-permute-start.10 = (bf16[512,384]{0,1:T(8,128)(2,1)S(1)}, bf16[512,384]{0,1:T(8,128)(2,1)S(1)}, u32[]{:S(2)}, u32[]{:S(2)}) collective-permute-start(bf16[512,384]{0,1:T(8,128)(2,1)S(1)} %get-tuple-element.11), channel_id=1, source_target_pairs={{0,1},{2,3},{4,5},{6,7},{8,9},{10,11},{12,13},{14,15},{16,17},{18,... | collective-permute-start | bytes 1179656 | tf_op jit(solution)/shard_map/ppermute | solution.py:10
  181.8 34.5 %collective-permute-start.11 = (bf16[512,384]{0,1:T(8,128)(2,1)S(1)}, bf16[512,384]{0,1:T(8,128)(2,1)S(1)}, u32[]{:S(2)}, u32[]{:S(2)}) collective-permute-start(bf16[512,384]{0,1:T(8,128)(2,1)S(1)} %get-tuple-element.10), channel_id=1, source_target_pairs={{1,0},{3,2},{5,4},{7,6},{9,8},{11,10},{13,12},{15,14},{17,16},{19,... | collective-permute-start | bytes 1179656 | tf_op jit(solution)/shard_map/ppermute | solution.py:10
  183.1 33.2 %collective-permute-start.8 = (bf16[512,384]{0,1:T(8,128)(2,1)S(1)}, bf16[512,384]{0,1:T(8,128)(2,1)S(1)}, u32[]{:S(2)}, u32[]{:S(2)}) collective-permute-start(bf16[512,384]{0,1:T(8,128)(2,1)S(1)} %get-tuple-element.9), channel_id=1, source_target_pairs={{0,2},{2,4},{4,6},{6,8},{8,10},{10,12},{12,14},{14,16},{16,18},{18... | collective-permute-start | bytes 1179656 | tf_op jit(solution)/shard_map/ppermute | solution.py:10
  187.4 28.9 %collective-permute-start.9 = (bf16[512,384]{0,1:T(8,128)(2,1)S(1)}, bf16[512,384]{0,1:T(8,128)(2,1)S(1)}, u32[]{:S(2)}, u32[]{:S(2)}) collective-permute-start(bf16[512,384]{0,1:T(8,128)(2,1)S(1)} %get-tuple-element.12), channel_id=1, source_target_pairs={{2,0},{4,2},{6,4},{8,6},{10,8},{12,10},{14,12},{16,14},{18,16},{20... | collective-permute-start | bytes 1179656 | tf_op jit(solution)/shard_map/ppermute | solution.py:10
  188.8 16.4 %collective-permute-start.12 = (bf16[512]{0:T(512)(128)(2,1)S(1)}, bf16[512]{0:T(512)(128)(2,1)S(1)}, u32[]{:S(2)}, u32[]{:S(2)}) collective-permute-start(bf16[512]{0:T(512)(128)(2,1)S(1)} %get-tuple-element.5), channel_id=1, source_target_pairs={{0,2},{2,4},{4,6},{6,8},{8,10},{10,12},{12,14},{14,16},{16,18},{18... | collective-permute-start | bytes 3080 | tf_op jit(solution)/shard_map/ppermute | solution.py:10
  205.2 6.0 %collective-permute-start.13 = (bf16[512]{0:T(512)(128)(2,1)S(1)}, bf16[512]{0:T(512)(128)(2,1)S(1)}, u32[]{:S(2)}, u32[]{:S(2)}) collective-permute-start(bf16[512]{0:T(512)(128)(2,1)S(1)} %get-tuple-element.6), channel_id=1, source_target_pairs={{2,0},{4,2},{6,4},{8,6},{10,8},{12,10},{14,12},{16,14},{18,16},{20... | collective-permute-start | bytes 3080 | tf_op jit(solution)/shard_map/ppermute | solution.py:10
  211.1 2.1 collective-permute-start.14
  213.2 3.0 %collective-permute-start.15 = (bf16[512]{0:T(512)(128)(2,1)S(1)}, bf16[512]{0:T(512)(128)(2,1)S(1)}, u32[]{:S(2)}, u32[]{:S(2)}) collective-permute-start(bf16[512]{0:T(512)(128)(2,1)S(1)} %get-tuple-element.7), channel_id=1, source_target_pairs={{1,0},{3,2},{5,4},{7,6},{9,8},{11,10},{13,12},{15,14},{17,16},{19,... | collective-permute-start | bytes 3080 | tf_op jit(solution)/shard_map/ppermute | solution.py:10
Sparse Core Ops, SparseCore 0:
  27.7 126.7 all-reduce.1
where the time goes:
time: 230 us; the launch traced here: 225 us
  waiting for transfers between devices  157 us (68%)
  starting transfers between devices  33.8 us (15%)
  matrix products  15.1 us (7%)
  between operations  13.7 us (6%)
    psum x1, waiting for transfers between devices, local(): lax.psum(jnp.einsum('cl,cr->lr', level_phi, assembled, precision=highest)...  125 us
    ppermute x12, starting transfers between devices, passed_along(): return lax.ppermute(block, axis, route)  26.5 us
    ppermute x12, waiting for transfers between devices, passed_along(): return lax.ppermute(block, axis, route)  25.7 us
    dot_general x1, matrix products, local(): jnp.dot(local_inverse[0, 0], masked, preferred_element_type=jnp.float32)  7.52 us
    ppermute x2, waiting for transfers between devices, extended(): lax.ppermute(lax.slice_in_dim(block, 0, width, axis=dim), axis, backward)  6.18 us
    ppermute x2, starting transfers between devices, extended(): lax.ppermute(lax.slice_in_dim(block, block.shape[dim] - width, None, axis...  4.67 us
  transfers between devices with their start and end apart: 17, of which 11 were waited for; matrix products, arithmetic and copies ran while one was open for 0% of the time, Pallas kernels for 0%

commit v1 on v0

v1 whole, which is shorter than its diff:
```python
import functools

import jax
import jax.numpy as jnp
from jax import lax
from jax.experimental import pallas as pl
from jax.experimental.pallas import tpu as pltpu
from jax.sharding import PartitionSpec as P

BF = jnp.bfloat16
F32 = jnp.float32
I32 = jnp.int32
INVERSE_LANE = 128
VMEM = pltpu.VMEM
SMEM = pltpu.SMEM


def near_pairs(count):
    return [(i, i ^ 1) for i in range(count) if i ^ 1 < count]


def far_pairs(count):
    return [(i, i + 1 if i % 2 else i - 1) for i in range(1, count) if i % 2 == 0 or i + 1 < count]


def swapped(block, axis, pairs):
    return lax.ppermute(block, axis, pairs) if pairs else jnp.zeros_like(block)


def dot(a, b):
    return jnp.dot(a.astype(BF), b.astype(BF), preferred_element_type=F32)


def tdot(a, b):
    return lax.dot_general(
        a.astype(BF), b.astype(BF), (((0,), (0,)), ((), ())), preferred_element_type=F32
    )


def whole(spaces):
    return [pl.BlockSpec(memory_space=space) for space in spaces]


def call(body, outs, inputs, flops=1 << 22):
    spaces = [SMEM] + [VMEM] * (len(inputs) - 1)
    return pl.pallas_call(
        body,
        out_shape=[jax.ShapeDtypeStruct(shape, kind) for shape, kind in outs],
        in_specs=whole(spaces),
        out_specs=whole([VMEM] * len(outs)),
        cost_estimate=pl.CostEstimate(flops=flops, bytes_accessed=1 << 20, transcendentals=0),
        compiler_params=pltpu.CompilerParams(vmem_limit_bytes=6 << 20),
    )(*inputs)


class Sizes:
    pass


def slot_row(block):
    rows = block.astype(F32)
    return (rows[0:1] * 16.0 + rows[1:2]).astype(I32)


def face_slice(ref, index, face):
    return ref[:, pl.ds(pl.multiple_of(index * face, 128), face)]


def pack_small(z, info, slots, level, inverse, out):
    out[0 : z.coarse, :] = jnp.zeros((z.coarse, z.span), BF)
    out[0 : z.coarse, 0 : z.top] = level[...].astype(BF)
    out[0 : z.coarse, INVERSE_LANE : INVERSE_LANE + z.block] = inverse[...].astype(BF)


def pack_marks(z, slots, stiff, out, base):
    row = lax.broadcasted_iota(I32, (16, z.span), 0)
    full = jnp.where(row == 2, stiff.astype(F32), 0.0)
    out[base : base + 16, :] = full.astype(BF)
    value = slots[...]
    high = lax.shift_right_logical(value, 4)
    low = value - high * 16
    row = lax.broadcasted_iota(I32, (16, z.primal), 0)
    marks = jnp.where(row == 0, high, jnp.where(row == 1, low, 0)).astype(F32)
    out[base : base + 16, 0 : z.primal] = jnp.where(row == 2, full[:, : z.primal], marks).astype(BF)


def pack_line(z, info, phi, stiff, slots, level, inverse, *outs):
    yodd = info[5] % 2
    pack_small(z, info, slots, level, inverse, outs[0])
    pack_marks(z, slots, face_slice(stiff, 3 - yodd, z.face), outs[0], z.coarse)
    base = z.coarse + 16
    outs[0][base : base + z.primal, :] = face_slice(phi, 3 - yodd, z.face)
    if len(outs) > 1:
        outs[1][0 : z.primal, :] = face_slice(phi, 2 + yodd, z.face)
        pack_marks(z, slots, face_slice(stiff, 2 + yodd, z.face), outs[1], z.primal)


def pack_sides(z, info, phi, stiff, slots, *refs):
    line, (to_a, to_b) = refs[:-2], refs[-2:]
    odd = info[4]
    to_a[0 : z.primal, :] = face_slice(phi, 1 - odd, z.face)
    pack_marks(z, slots, face_slice(stiff, 1 - odd, z.face), to_a, z.primal)
    base = z.primal + 16
    for y in range(z.ny):
        to_a[base + y * z.coarse : base + (y + 1) * z.coarse, :] = small_of(z, line, y)
    to_b[0 : z.primal, :] = face_slice(phi, odd, z.face)
    pack_marks(z, slots, face_slice(stiff, odd, z.face), to_b, z.primal)


def small_of(z, line, y):
    return line[y][0 : z.coarse, :] if z.paired else line[0][y, 0 : z.coarse, :]


def marks_of(z, line, y):
    if z.paired:
        return line[y][z.coarse : z.coarse + 16, 0 : z.primal]
    return line[0][y, z.coarse : z.coarse + 16, 0 : z.primal]


def row_of(z, slot, y, own_y, place):
    side_x = slot // (3 * z.coarse)
    rest = slot - side_x * (3 * z.coarse)
    side_y = rest // z.coarse
    target = y + side_y - 1
    order = (target + own_y) % 2 if z.paired else target
    row = place(side_x - 1) * z.line + order * z.coarse + rest - side_y * z.coarse
    return jnp.where((target >= 0) & (target < z.ny), row, -1)


def one_hot(rows, count):
    return (lax.broadcasted_iota(I32, (count, rows.shape[1]), 0) == rows).astype(F32).astype(BF)


def spread_body(z, info, *refs):
    line, partial, (to_b, to_a, middle) = refs[: z.lines], refs[z.lines : -3], refs[-3:]
    own_y = info[5]
    total = jnp.zeros((3 * z.line, z.vectors), F32)
    for y in range(z.ny):
        at = (own_y + y) % 2 if z.paired else y
        rows = row_of(z, slot_row(marks_of(z, line, y)), at, own_y, lambda side: side + 1)
        block = partial[y][...] if z.paired else partial[0][y]
        total += dot(one_hot(rows, 3 * z.line), block)
    down, up = total[: z.line], total[2 * z.line :]
    even = info[4] == 0
    to_b[...] = jnp.where(even, down, up).astype(BF)
    to_a[...] = jnp.where(even, up, down).astype(BF)
    middle[...] = total[z.line : 2 * z.line]


def level_line(z, line):
    return jnp.concatenate([small_of(z, line, y)[:, : z.top] for y in range(z.ny)], axis=0)


def top_body(z, info, *refs):
    line = refs[: z.lines]
    side_a, came, to_a, middle, message, top_part, kept = refs[z.lines :]
    value = middle[...] + came[...].astype(F32)
    base = z.primal + 16
    level_a = side_a[base : base + z.line, 0 : z.top]
    part = tdot(level_line(z, line), value) + tdot(level_a, to_a[...])
    top_part[...] = part
    kept[...] = value
    message[0 : z.top, :] = part.astype(BF)
    message[z.top : z.top + z.line, :] = to_a[...]
    message[z.top + z.line :, :] = value.astype(BF)


def coarse_body(z, info, *refs):
    line = refs[: z.lines]
    side_a, answer, top_part, kept, to_a, total, total_sent, beyond = refs[z.lines :]
    summed = top_part[...] + answer[0 : z.top, :].astype(F32)
    total[...] = summed
    total_sent[...] = summed.astype(BF)
    own = kept[...] + answer[z.top : z.top + z.line, :].astype(F32)
    other = to_a[...].astype(F32) + answer[z.top + z.line :, :].astype(F32)

    def ordered(block):
        if not z.paired:
            return block
        turned = jnp.concatenate([block[z.coarse :], block[: z.coarse]], axis=0)
        return jnp.where(info[5] == 0, block, turned)

    base = z.primal + 16
    beyond[0 : z.line, :] = dot(
        side_a[base : base + z.line, INVERSE_LANE : INVERSE_LANE + z.block], ordered(other)
    ).astype(BF)
    inverse = jnp.concatenate(
        [small_of(z, line, y)[:, INVERSE_LANE : INVERSE_LANE + z.block] for y in range(z.ny)], axis=0
    )
    beyond[z.line : 2 * z.line, :] = dot(inverse, ordered(own)).astype(BF)
    beyond[2 * z.line :, :] = jnp.zeros((z.line, z.vectors), BF)
    beyond[2 * z.line :, 0 : z.top] = level_line(z, line)
    beyond[2 * z.line :, INVERSE_LANE : INVERSE_LANE + z.top] = side_a[base : base + z.line, 0 : z.top]


def values_body(z, info, *refs):
    line = refs[: z.lines]
    side_a, side_b, beyond, come, over, top_inverse, near, top_map = refs[z.lines :]
    own_y = info[5]
    sign = 1 - 2 * info[4]
    first, second, third = slice(0, z.line), slice(z.line, 2 * z.line), slice(2 * z.line, 3 * z.line)
    late = slice(INVERSE_LANE, INVERSE_LANE + z.top)
    coarse = jnp.concatenate(
        [come[first], come[second], beyond[second], beyond[first], over[second]], axis=0
    )
    levels = jnp.concatenate(
        [
            come[third, late],
            come[third, 0 : z.top],
            beyond[third, 0 : z.top],
            beyond[third, late],
            over[third, 0 : z.top],
        ],
        axis=0,
    )
    levels = dot(levels, top_inverse[...])
    marks = slice(z.primal, z.primal + 16)
    wanted = [
        (None, own_y, 0),
        (side_a[marks, 0 : z.primal], own_y, 1),
        (side_b[marks, 0 : z.primal], own_y, -1),
    ]
    if z.paired:
        wanted[0] = (marks_of(z, line, 0), own_y, 0)
        wanted.append((marks_of(z, line, 1), 1 - own_y, 0))
    else:
        wanted[0] = (line[0][own_y, z.coarse : z.coarse + 16, 0 : z.primal], own_y, 0)
        yodd = own_y % 2
        for shift in (1 - 2 * yodd, 2 * yodd - 1):
            other = jnp.clip(own_y + shift, 0, z.ny - 1)
            wanted.append((line[0][other, z.coarse : z.coarse + 16, 0 : z.primal], other, 0))
    for i, (block, y, at) in enumerate(wanted):
        rows = row_of(z, slot_row(block), y, own_y, lambda side: sign * side + at + 2)
        chosen = one_hot(rows, 5 * z.line)
        near[i * z.primal : (i + 1) * z.primal, :] = tdot(chosen, coarse)
        top_map[i * z.primal : (i + 1) * z.primal, :] = tdot(chosen, levels).astype(BF)


def spread_column(row, count):
    high = row.astype(BF)
    low = (row - high.astype(F32)).astype(BF)
    at = lax.broadcasted_iota(I32, (16, row.shape[1]), 0)
    pair = jnp.where(at == 0, high.astype(F32), jnp.where(at == 1, low.astype(F32), 0.0))
    return tdot(pair, jnp.ones((16, count), F32))


def weighted_body(z, info, which, inverse, masked, stiff, out):
    value = dot(inverse[...], masked[...])
    out[...] = (value * spread_column(stiff[...].astype(F32), z.vectors)).astype(BF)


def weighted_face(z, inverse, masked, stiff, info, index):
    tiles = 2
    rows = z.face // tiles
    return pl.pallas_call(
        functools.partial(weighted_body, z),
        out_shape=jax.ShapeDtypeStruct((z.face, z.vectors), BF),
        grid_spec=pltpu.PrefetchScalarGridSpec(
            num_scalar_prefetch=2,
            grid=(tiles,),
            in_specs=[
                pl.BlockSpec((rows, z.rows), lambda i, info, which: (which[0] * tiles + i, 0)),
                pl.BlockSpec((z.rows, z.vectors), lambda i, info, which: (0, 0)),
                pl.BlockSpec((1, rows), lambda i, info, which: (0, which[0] * tiles + i)),
            ],
            out_specs=pl.BlockSpec((rows, z.vectors), lambda i, info, which: (i, 0)),
        ),
        cost_estimate=pl.CostEstimate(
            flops=2 * z.face * z.rows * z.vectors,
            bytes_accessed=2 * z.face * z.rows,
            transcendentals=0,
        ),
        compiler_params=pltpu.CompilerParams(vmem_limit_bytes=12 << 20),
    )(info, index, inverse, masked, stiff)


def final_body(z, info, order, phi, stiff, near, top_map, total, came, *refs):
    given, (out, values) = refs[:-2], refs[-2:]
    step = pl.program_id(0)

    @pl.when(step == 0)
    def _():
        top = total[...] + came[...].astype(F32)
        values[...] = (near[...] + dot(top_map[...], top)).astype(BF)

    for side in range(4):

        @pl.when(step == side)
        def _(side=side):
            own = given[side]
            stiff_row = stiff[...].astype(F32)
            value = own[...].astype(F32)
            value += tdot(phi[...].astype(F32) * stiff_row, values[0 : z.primal, :])
            scale = stiff_row
            if side < z.sides:
                got, static = given[4 + side], given[4 + z.sides + side]
                base = z.phi_base[side]
                mark = z.mark_base[side]
                other_row = static[mark : mark + 16, :].astype(F32)[2:3, :]
                value += got[...].astype(F32)
                value += tdot(
                    static[base : base + z.primal, :].astype(F32) * other_row,
                    values[(1 + side) * z.primal : (2 + side) * z.primal, :],
                )
                scale = scale + other_row
            value = value * spread_column(1.0 / scale, z.vectors)
            live = lax.broadcasted_iota(I32, value.shape, 0) < info[order[side]]
            out[...] = jnp.where(live, value, 0.0).astype(BF)


def local(
    residual,
    local_inverse,
    primal_basis,
    row_stiffness,
    face_sizes,
    primal_slots,
    block_inverse,
    level_basis,
    top_inverse,
):
    nx, ny = lax.axis_size("gx"), lax.axis_size("gy")
    odd = lax.axis_index("gx") % 2
    own_y = lax.axis_index("gy")
    yodd = own_y % 2
    near_x, far_x = near_pairs(nx), far_pairs(nx)
    near_y, far_y = near_pairs(ny), far_pairs(ny)

    z = Sizes()
    own_rows = residual[0, 0]
    phi = primal_basis[0, 0]
    stiff = row_stiffness[0]
    slots = primal_slots[0]
    z.ny, z.paired = ny, ny == 2
    z.rows, z.vectors = own_rows.shape
    z.face = z.rows // 4
    z.primal = phi.shape[0]
    z.coarse, z.block = block_inverse.shape[2:]
    z.top = level_basis.shape[3]
    z.line = ny * z.coarse
    z.lines = 2 if z.paired else 1
    z.span = z.face
    z.sides = 3 if z.paired else 4
    counts = face_sizes[0, 0]
    at = jnp.arange(8, dtype=I32)
    info = jnp.where(at == 4, odd, jnp.where(at == 5, own_y, jnp.pad(counts, (0, 4))))

    bound = functools.partial
    marked = z.coarse + 16
    outs = [((marked + z.primal, z.span), BF)]
    if far_y:
        outs.append(((z.primal + 16, z.span), BF))
    packed = call(
        bound(pack_line, z), outs, [info, phi, stiff, slots, level_basis[0, 0], block_inverse[0, 0]]
    )
    if z.paired:
        other = swapped(packed[0], "gy", near_y)
        line = [packed[0], other]
        y_static = [other]
        z.phi_base, z.mark_base = [0, 0, marked], [z.primal, z.primal, z.coarse]
    else:
        line = [lax.all_gather(packed[0][:marked], "gy", axis=0)]
        y_static = [swapped(packed[0], "gy", near_y)]
        z.phi_base, z.mark_base = [0, 0, marked, 0], [z.primal, z.primal, z.coarse, z.primal]
        y_static.append(swapped(packed[1], "gy", far_y) if far_y else jnp.zeros((z.primal + 16, z.span), BF))

    sent_a, sent_b = call(
        bound(pack_sides, z),
        [((z.primal + 16 + z.line, z.span), BF), ((z.primal + 16, z.span), BF)],
        [info, phi, stiff, slots] + line,
    )
    side_a = swapped(sent_a, "gx", near_x)
    side_b = swapped(sent_b, "gx", far_x)

    position = jnp.arange(z.rows, dtype=I32)
    picked = jnp.where(
        (position // z.face)[:, None] == jnp.arange(4, dtype=I32)[None, :], counts[None, :], 0
    )
    live = (position % z.face < jnp.sum(picked, axis=1))[:, None]
    masked = jnp.where(live, own_rows, jnp.zeros((), BF))
    partial = jnp.dot(phi, masked, preferred_element_type=F32).astype(BF)
    if z.paired:
        partial_line = [partial, swapped(partial, "gy", near_y)]
    else:
        partial_line = [lax.all_gather(partial, "gy", axis=0)]
    wide = (z.line, z.vectors)
    to_b, to_a, middle = call(
        bound(spread_body, z), [(wide, BF), (wide, BF), (wide, F32)], [info] + line + partial_line
    )
    came = swapped(to_b, "gx", far_x)
    message, top_part, kept = call(
        bound(top_body, z),
        [((z.top + 2 * z.line, z.vectors), BF), ((z.top, z.vectors), F32), (wide, F32)],
        [info] + line + [side_a, came, to_a, middle],
    )
    answer = swapped(message, "gx", near_x)
    total, total_sent, beyond = call(
        bound(coarse_body, z),
        [
            ((z.top, z.vectors), F32),
            ((z.top, z.vectors), BF),
            ((3 * z.line, z.vectors), BF),
        ],
        [info] + line + [side_a, answer, top_part, kept, to_a],
    )
    come = swapped(beyond, "gx", far_x)
    over = swapped(come, "gx", near_x)
    arrived = jnp.zeros((z.top, z.vectors), BF)
    step = 2
    while step < nx:
        if step > 2:
            total = total + arrived
            total_sent = total.astype(BF)
        arrived = lax.ppermute(total_sent, "gx", [(i, i ^ step) for i in range(nx)])
        step *= 2

    count = 1 + z.sides
    near, top_map = call(
        bound(values_body, z),
        [((count * z.primal, z.vectors), F32), ((count * z.primal, z.top), BF)],
        [info] + line + [side_a, side_b, beyond, come, over, top_inverse],
    )

    order = jnp.where(
        at == 0, 1 - odd, jnp.where(at == 1, odd, jnp.where(at == 2, 3 - yodd, 2 + yodd))
    )
    pairs = [("gx", near_x), ("gx", far_x), ("gy", near_y), ("gy", far_y)]
    own = [weighted_face(z, local_inverse[0, 0], masked, stiff, info, order[i : i + 1]) for i in range(4)]
    got = [swapped(own[i], *pairs[i]) for i in range(z.sides)]

    static = [side_a, side_b] + y_static
    fixed = lambda i, info, order: (0, 0)
    full = lambda item: pl.BlockSpec(item.shape, fixed)
    given = own + got + static
    result = pl.pallas_call(
        bound(final_body, z),
        out_shape=jax.ShapeDtypeStruct((z.rows, z.vectors), BF),
        grid_spec=pltpu.PrefetchScalarGridSpec(
            num_scalar_prefetch=2,
            grid=(4,),
            in_specs=[
                pl.BlockSpec((z.primal, z.face), lambda i, info, order: (0, order[i])),
                pl.BlockSpec((1, z.face), lambda i, info, order: (0, order[i])),
            ]
            + [full(item) for item in [near, top_map, total, arrived] + given],
            out_specs=pl.BlockSpec((z.face, z.vectors), lambda i, info, order: (order[i], 0)),
            scratch_shapes=[pltpu.VMEM((count * z.primal, z.vectors), BF)],
        ),
        cost_estimate=pl.CostEstimate(flops=1 << 30, bytes_accessed=1 << 22, transcendentals=0),
        compiler_params=pltpu.CompilerParams(vmem_limit_bytes=16 << 20),
    )(info, order, phi, stiff, near, top_map, total, arrived, *given)
    return result[None, None]


def solution(mesh):
    in_specs = (
        P("gx", "gy", None, None),
        P("gx", "gy", None, None),
        P("gx", "gy", None, None),
        P("gx", "gy", None),
        P("gx", "gy", None),
        P("gx", "gy", None),
        P("gx", "gy", None, None),
        P("gx", "gy", None, None),
        P(),
    )
    out_specs = P("gx", "gy", None, None)
    return jax.shard_map(local, mesh=mesh, in_specs=in_specs, out_specs=out_specs, check_vma=False)
```

time: 230 us -> 69.4 us (0.30); the launches traced: 225 us -> 69 us
  waiting for transfers between devices: 157 us -> 4.7 us
  Pallas kernels: 0 us -> 19.4 us
  between operations: 13.7 us -> 0.34 us
  matrix products: 15.1 us -> 2.1 us
  local copies, waits for them, and re-layouts: 1.96 us -> 4.51 us
    psum x1 -> x0, waiting for transfers between devices: 125 us -> none  [local(): lax.psum(jnp.einsum('cl,cr->lr', level_phi, assembled, precision=highest)...]
    ppermute x16 -> x14, waiting for transfers between devices: 32.3 us -> 4.7 us  [the longest x11 2.63 us: swapped(): return lax.ppermute(block, axis, pairs) if pairs else jnp.zeros_like(block)]
    pallas_call x0 -> x11, Pallas kernels: none -> 19.4 us  [the longest x4 11.1 us: weighted_face(): pl.pallas_call(functools.partial(weighted_body, z), out_shape=jax.ShapeDt...]
    dot_general x9 -> x1, matrix products: 15.1 us -> 2.1 us  [local(): partial = jnp.dot(phi, masked, preferred_element_type=F32).astype(BF)]
    unnamed x14 -> x18, local copies, waits for them, and re-layouts: 0.2 us -> 3.85 us
    ppermute x16 -> x14, starting transfers between devices: 33.8 us -> 35.5 us  [the longest x3 19.8 us: local(): arrived = lax.ppermute(total_sent, 'gx', [(i, i ^ step) for i in range(nx)])]
  transfers between devices with their start and end apart: 17 -> 14, of which waited for: 11 -> 2; matrix products, arithmetic and copies ran while one was open for 0% -> 3% of each run, Pallas kernels for 0% -> 22%
where the time goes in v1:
time: 69.4 us; the launch traced here: 69 us
  starting transfers between devices  35.5 us (51%)
  Pallas kernels  19.4 us (28%)
  waiting for transfers between devices  4.7 us (7%)
  local copies, waits for them, and re-layouts  4.51 us (6%)
  other arithmetic  2.47 us (4%)
  matrix products  2.1 us (3%)
    ppermute x3, starting transfers between devices, local(): arrived = lax.ppermute(total_sent, 'gx', [(i, i ^ step) for i in range(nx)])  19.8 us
    ppermute x11, starting transfers between devices, swapped(): return lax.ppermute(block, axis, pairs) if pairs else jnp.zeros_like(block)  15.7 us
    pallas_call x4, Pallas kernels, weighted_face(): pl.pallas_call(functools.partial(weighted_body, z), out_shape=jax.ShapeDt...  11.1 us
    pallas_call x6, Pallas kernels, call(): pl.pallas_call(body, out_shape=[jax.ShapeDtypeStruct(shape, kind) for sha...  4.49 us
    unnamed x18, local copies, waits for them, and re-layouts  3.85 us
    pallas_call x1, Pallas kernels, local(): pl.pallas_call(bound(final_body, z), out_shape=jax.ShapeDtypeStruct((z.ro...  3.77 us
    ppermute x11, waiting for transfers between devices, swapped(): return lax.ppermute(block, axis, pairs) if pairs else jnp.zeros_like(block)  2.63 us
    dot_general x1, matrix products, local(): partial = jnp.dot(phi, masked, preferred_element_type=F32).astype(BF)  2.1 us
  transfers between devices with their start and end apart: 14, of which 2 were waited for; matrix products, arithmetic and copies ran while one was open for 3% of the time, Pallas kernels for 22%

profile of v1, /device:TPU:0, one launch (start us, length us, event | category | flops | bytes accessed | tf_op | source)
XLA Modules:
  0.0 69.0 jit_solution(9351685801619326341)
XLA Ops:
  0.0 0.8 %select_reduce_fusion = s32[2048]{0:T(1024)S(1)} fusion(s32[4]{0:T(128)} %bitcast.39, s32[2048]{0:T(1024)S(1)} %add_select_fusion), kind=kLoop, calls=%fused_computation.11 | loop fusion | flops 22528 | bytes 16400 | tf_op jit(solution)/shard_map/reduce_sum | solution.py:379
  0.9 2.1 %fusion.7.refs_2_ = bf16[96,384]{1,0:T(8,128)(2,1)S(1)} fusion(bf16[1,1,2048,384]{3,2,1,0:T(8,128)(2,1)} %param.9, pred[2048]{0:T(1024)(128)(4,1)S(1)} %fusion.12, bf16[1,1,96,2048]{3,2,1,0:T(8,128)(2,1)} %param.11), kind=kOutput, calls=%fused_computation.6 | convolution fusion | flops 151818240 | bytes 2041856 | tf_op jit(solution)/shard_map/dot_general | solution.py:381
  3.0 0.6 collective-permute-start.3
  3.6 0.6 shard_map.91.refs_0_
  4.2 0.1 collective-permute-start
  4.3 1.6 %bitcast_select_fusion.masked = bf16[2048,384]{1,0:T(8,128)(2,1)S(1)} fusion(bf16[1,1,2048,384]{3,2,1,0:T(8,128)(2,1)} %param.9, pred[2048]{0:T(1024)(128)(4,1)S(1)} %fusion.12), kind=kLoop, calls=%fused_computation | loop fusion | flops 786432 | bytes 3147776 | tf_op jit(solution)/shard_map/jit(_where)/select_n | solution.py:380
  5.9 0.6 shard_map.92
  6.5 3.0 %collective-permute-start.1 = (bf16[176,512]{1,0:T(8,128)(2,1)S(1)}, bf16[176,512]{1,0:T(8,128)(2,1)S(1)}, u32[]{:S(2)}, u32[]{:S(2)}) collective-permute-start(bf16[176,512]{1,0:T(8,128)(2,1)S(1)} %get-tuple-element.18), channel_id=1, source_target_pairs={{0,2},{2,0},{4,6},{6,4},{8,10},{10,8},{12,14},{14,12},{16,18},{18,... | collective-permute-start | bytes 540680 | tf_op jit(solution)/shard_map/ppermute | solution.py:27
  9.5 0.8 %shard_map.93 = (bf16[64,384]{1,0:T(8,128)(2,1)S(1)}, bf16[64,384]{1,0:T(8,128)(2,1)S(1)}, f32[64,384]{1,0:T(8,128)S(1)}) custom-call(s32[8]{0:T(128)S(1)} %compare_select_fusion.4.info, bf16[144,512]{1,0:T(8,128)(2,1)S(1)} %shard_map.91.refs_0_, bf16[144,512]{1,0:T(8,128)(2,1)S(1)} %collective-permute-done.refs_1_.refs_9_, ...), custom_call_target="tpu_custom_call" | custom-call | flops 4194304 | bytes 1048576 | tf_op jit(solution)/shard_map/pallas_call | solution.py:46
  10.3 0.7 collective-permute-start.4
  11.0 0.7 fusion.21
  11.7 2.6 %collective-permute-done.1.refs_2_.refs_7_ = bf16[176,512]{1,0:T(8,128)(2,1)S(1)} collective-permute-done((bf16[176,512]{1,0:T(8,128)(2,1)S(1)}, bf16[176,512]{1,0:T(8,128)(2,1)S(1)}, u32[]{:S(2)}, u32[]{:S(2)}) %collective-permute-start.1) | collective-permute-done | bytes 180256 | tf_op jit(solution)/shard_map/ppermute | solution.py:27
  14.3 0.7 %shard_map.94 = (bf16[192,384]{1,0:T(8,128)(2,1)S(1)}, f32[64,384]{1,0:T(8,128)S(1)}, f32[64,384]{1,0:T(8,128)S(1)}) custom-call(s32[8]{0:T(128)S(1)} %compare_select_fusion.4.info, bf16[144,512]{1,0:T(8,128)(2,1)S(1)} %shard_map.91.refs_0_, bf16[144,512]{1,0:T(8,128)(2,1)S(1)} %collective-permute-done.refs_1_.refs_9_, ...), custom_call_target="tpu_custom_call" | custom-call | flops 4194304 | bytes 1048576 | tf_op jit(solution)/shard_map/pallas_call | solution.py:46
  15.0 3.8 %collective-permute-start.5 = (bf16[192,384]{1,0:T(8,128)(2,1)S(1)}, bf16[192,384]{1,0:T(8,128)(2,1)S(1)}, u32[]{:S(2)}, u32[]{:S(2)}) collective-permute-start(bf16[192,384]{1,0:T(8,128)(2,1)S(1)} %get-tuple-element.23), channel_id=1, source_target_pairs={{0,2},{2,0},{4,6},{6,4},{8,10},{10,8},{12,14},{14,12},{16,18},{18,... | collective-permute-start | bytes 442376 | tf_op jit(solution)/shard_map/ppermute | solution.py:27
  18.8 3.4 %copy-done = bf16[1,1,2048,2048]{3,2,1,0:T(8,128)(2,1)S(1)} copy-done((bf16[1,1,2048,2048]{3,2,1,0:T(8,128)(2,1)S(1)}, bf16[1,1,2048,2048]{3,2,1,0:T(8,128)(2,1)}, u32[]{:S(2)}) %copy-start) | copy-done | bytes 8388632
  22.2 2.9 %shard_map.97.refs_0_ = bf16[512,384]{1,0:T(8,128)(2,1)S(1)} custom-call(s32[8]{0:T(128)S(1)} %compare_select_fusion.4.info, s32[1]{0:T(128)} %get-tuple-element.36.which, bf16[2048,2048]{1,0:T(8,128)(2,1)S(1)} %bitcast.21, bf16[2048,384]{1,0:T(8,128)(2,1)S(1)} %bitcast_select_fusion.masked, bf16[1,2048]{1,0:T(2,128)(2,1)S(1)} %bitcast.30), custom_call_target="tpu_custom_call" | custom-call | flops 805306368 | bytes 2097152 | tf_op jit(solution)/shard_map/pallas_call | solution.py:255
  25.1 0.1 collective-permute-start.11
  25.2 0.4 copy-done.1
  25.6 2.8 %shard_map.98.refs_1_ = bf16[512,384]{1,0:T(8,128)(2,1)S(1)} custom-call(s32[8]{0:T(128)S(1)} %compare_select_fusion.4.info, s32[1]{0:T(128)} %get-tuple-element.35.which, bf16[2048,2048]{1,0:T(8,128)(2,1)S(1)} %bitcast.22, bf16[2048,384]{1,0:T(8,128)(2,1)S(1)} %bitcast_select_fusion.masked, bf16[1,2048]{1,0:T(2,128)(2,1)S(1)} %bitcast.31), custom_call_target="tpu_custom_call" | custom-call | flops 805306368 | bytes 2097152 | tf_op jit(solution)/shard_map/pallas_call | solution.py:255
  28.4 0.7 collective-permute-start.12
  29.1 0.7 %shard_map.95 = (f32[64,384]{1,0:T(8,128)S(1)}, bf16[64,384]{1,0:T(8,128)(2,1)S(1)}, bf16[192,384]{1,0:T(8,128)(2,1)S(1)}) custom-call(s32[8]{0:T(128)S(1)} %compare_select_fusion.4.info, bf16[144,512]{1,0:T(8,128)(2,1)S(1)} %shard_map.91.refs_0_, bf16[144,512]{1,0:T(8,128)(2,1)S(1)} %collective-permute-done.refs_1_.refs_9_, ...), custom_call_target="tpu_custom_call" | custom-call | flops 4194304 | bytes 1048576 | tf_op jit(solution)/shard_map/pallas_call | solution.py:46
  29.8 4.3 %collective-permute-start.8 = (bf16[64,384]{1,0:T(8,128)(2,1)S(1)}, bf16[64,384]{1,0:T(8,128)(2,1)S(1)}, u32[]{:S(2)}, u32[]{:S(2)}) collective-permute-start(bf16[64,384]{1,0:T(8,128)(2,1)S(1)} %get-tuple-element.30), channel_id=1, source_target_pairs={{0,4},{2,6},{4,0},{6,2},{8,12},{10,14},{12,8},{14,10},{16,20},{18,... | collective-permute-start | bytes 147464 | tf_op jit(solution)/shard_map/ppermute | solution.py:414
  34.2 2.8 %shard_map.99.refs_2_ = bf16[512,384]{1,0:T(8,128)(2,1)S(1)} custom-call(s32[8]{0:T(128)S(1)} %compare_select_fusion.4.info, s32[1]{0:T(128)} %get-tuple-element.34.which, bf16[2048,2048]{1,0:T(8,128)(2,1)S(1)} %bitcast.23, bf16[2048,384]{1,0:T(8,128)(2,1)S(1)} %bitcast_select_fusion.masked, bf16[1,2048]{1,0:T(2,128)(2,1)S(1)} %bitcast.32), custom_call_target="tpu_custom_call" | custom-call | flops 805306368 | bytes 2097152 | tf_op jit(solution)/shard_map/pallas_call | solution.py:255
  37.0 0.7 collective-permute-start.6
  37.7 9.9 %collective-permute-start.9 = (bf16[64,384]{1,0:T(8,128)(2,1)S(1)}, bf16[64,384]{1,0:T(8,128)(2,1)S(1)}, u32[]{:S(2)}, u32[]{:S(2)}) collective-permute-start(bf16[64,384]{1,0:T(8,128)(2,1)S(1)} %fusion.11), channel_id=1, source_target_pairs={{0,8},{2,10},{4,12},{6,14},{8,0},{10,2},{12,4},{14,6},{16,24},{18,... | collective-permute-start | bytes 147464 | tf_op jit(solution)/shard_map/ppermute | solution.py:414
  47.6 2.1 %collective-permute-done.9 = bf16[64,384]{1,0:T(8,128)(2,1)S(1)} collective-permute-done((bf16[64,384]{1,0:T(8,128)(2,1)S(1)}, bf16[64,384]{1,0:T(8,128)(2,1)S(1)}, u32[]{:S(2)}, u32[]{:S(2)}) %collective-permute-start.9) | collective-permute-done | bytes 49184 | tf_op jit(solution)/shard_map/ppermute | solution.py:414
  49.6 0.7 collective-permute-start.2
  50.3 5.4 %collective-permute-start.7 = (bf16[192,384]{1,0:T(8,128)(2,1)S(1)}, bf16[192,384]{1,0:T(8,128)(2,1)S(1)}, u32[]{:S(2)}, u32[]{:S(2)}) collective-permute-start(bf16[192,384]{1,0:T(8,128)(2,1)S(1)} %collective-permute-done.6.refs_5_), channel_id=1, source_target_pairs={{0,2},{2,0},{4,6},{6,4},{8,10},{10,8},{12,14},{14,12},{16,18},{18,... | collective-permute-start | bytes 442376 | tf_op jit(solution)/shard_map/ppermute | solution.py:27
  55.7 5.6 %collective-permute-start.10 = (bf16[64,384]{1,0:T(8,128)(2,1)S(1)}, bf16[64,384]{1,0:T(8,128)(2,1)S(1)}, u32[]{:S(2)}, u32[]{:S(2)}) collective-permute-start(bf16[64,384]{1,0:T(8,128)(2,1)S(1)} %get-tuple-element.31), channel_id=1, source_target_pairs={{0,16},{2,18},{4,20},{6,22},{8,24},{10,26},{12,28},{14,30},{16,0},... | collective-permute-start | bytes 147464 | tf_op jit(solution)/shard_map/ppermute | solution.py:414
  61.3 2.7 %shard_map.100.refs_3_ = bf16[512,384]{1,0:T(8,128)(2,1)S(1)} custom-call(s32[8]{0:T(128)S(1)} %compare_select_fusion.4.info, s32[1]{0:T(128)} %get-tuple-element.33.which, bf16[2048,2048]{1,0:T(8,128)(2,1)S(1)} %bitcast.24, bf16[2048,384]{1,0:T(8,128)(2,1)S(1)} %bitcast_select_fusion.masked, bf16[1,2048]{1,0:T(2,128)(2,1)S(1)} %bitcast.33), custom_call_target="tpu_custom_call" | custom-call | flops 805306368 | bytes 2097152 | tf_op jit(solution)/shard_map/pallas_call | solution.py:255
  64.1 1.1 %shard_map.96 = (f32[384,384]{1,0:T(8,128)S(1)}, bf16[384,64]{1,0:T(8,128)(2,1)S(1)}) custom-call(s32[8]{0:T(128)S(1)} %compare_select_fusion.4.info, bf16[144,512]{1,0:T(8,128)(2,1)S(1)} %shard_map.91.refs_0_, bf16[144,512]{1,0:T(8,128)(2,1)S(1)} %collective-permute-done.refs_1_.refs_9_, bf16[176,512]{1,0:T(8,128)(2,1)S(1)} %collective-permute-done.1.refs_2_.refs_7_, ...), custom_call_target="tpu_custom_call" | custom-call | flops 4194304 | bytes 1048576 | tf_op jit(solution)/shard_map/pallas_call | solution.py:46
  65.2 3.8 %shard_map.101 = bf16[2048,384]{1,0:T(8,128)(2,1)} custom-call(s32[8]{0:T(128)S(1)} %compare_select_fusion.4.info, s32[8]{0:T(128)S(1)} %compare_select_fusion.2.order, bf16[96,2048]{1,0:T(8,128)(2,1)S(1)} %bitcast.27, bf16[1,2048]{1,0:T(2,128)(2,1)S(1)} %bitcast.34, f32[384,384]{1,0:T(8,128)S(1)} %get-tuple-element.27.near, ...), custom_call_target="tpu_custom_call" | custom-call | flops 1073741824 | bytes 4194304 | tf_op jit(solution)/shard_map/pallas_call | solution.py:435
  (35 shorter events, 0.2 us)
Async XLA Ops:
  0.0 3.6 %copy-start.8 = (s32[1,1,4]{2,1,0:T(1,128)S(1)}, s32[1,1,4]{2,1,0:T(1,128)}, u32[]{:S(2)}) copy-start(s32[1,1,4]{2,1,0:T(1,128)} %param.13) | copy-start | bytes 52
  0.8 2.7 %copy-start.2 = (bf16[1,1,96,2048]{3,2,1,0:T(8,128)(2,1)S(1)}, bf16[1,1,96,2048]{3,2,1,0:T(8,128)(2,1)}, u32[]{:S(2)}) copy-start(bf16[1,1,96,2048]{3,2,1,0:T(8,128)(2,1)} %param.11) | copy-start | bytes 1179652
  0.8 2.7 %copy-start.3 = (bf16[1,1,2048]{2,1,0:T(2,128)(2,1)S(1)}, bf16[1,1,2048]{2,1,0:T(2,128)(2,1)}, u32[]{:S(2)}) copy-start(bf16[1,1,2048]{2,1,0:T(2,128)(2,1)} %param.12) | copy-start | bytes 12292
  0.9 2.7 %copy-start.5 = (f32[1,1,32,64]{3,2,1,0:T(8,128)S(1)}, f32[1,1,32,64]{3,2,1,0:T(8,128)}, u32[]{:S(2)}) copy-start(f32[1,1,32,64]{3,2,1,0:T(8,128)} %param.16) | copy-start | bytes 24580
  0.9 2.7 %copy-start.6 = (f32[1,1,32,64]{3,2,1,0:T(8,128)S(1)}, f32[1,1,32,64]{3,2,1,0:T(8,128)}, u32[]{:S(2)}) copy-start(f32[1,1,32,64]{3,2,1,0:T(8,128)} %param.15) | copy-start | bytes 24580
  0.9 2.7 %copy-start.7 = (s32[1,1,96]{2,1,0:T(1,128)S(1)}, s32[1,1,96]{2,1,0:T(1,128)}, u32[]{:S(2)}) copy-start(s32[1,1,96]{2,1,0:T(1,128)} %param.14) | copy-start | bytes 1156
  3.0 6.5 %collective-permute-start.3 = (bf16[96,384]{1,0:T(8,128)(2,1)S(1)}, bf16[96,384]{1,0:T(8,128)(2,1)S(1)}, u32[]{:S(2)}, u32[]{:S(2)}) collective-permute-start(bf16[96,384]{1,0:T(8,128)(2,1)S(1)} %fusion.7.refs_2_), channel_id=1, source_target_pairs={{0,1},{1,0},{2,3},{3,2},{4,5},{5,4},{6,7},{7,6},{8,9},{9,8},{10,11... | collective-permute-start | bytes 221192 | tf_op jit(solution)/shard_map/ppermute | solution.py:27
  4.2 1.7 %collective-permute-start = (bf16[144,512]{1,0:T(8,128)(2,1)S(1)}, bf16[144,512]{1,0:T(8,128)(2,1)S(1)}, u32[]{:S(2)}, u32[]{:S(2)}) collective-permute-start(bf16[144,512]{1,0:T(8,128)(2,1)S(1)} %shard_map.91.refs_0_), channel_id=1, source_target_pairs={{0,1},{1,0},{2,3},{3,2},{4,5},{5,4},{6,7},{7,6},{8,9},{9,8},{10,11... | collective-permute-start | bytes 442376 | tf_op jit(solution)/shard_map/ppermute | solution.py:27
  6.5 7.8 %collective-permute-start.1 = (bf16[176,512]{1,0:T(8,128)(2,1)S(1)}, bf16[176,512]{1,0:T(8,128)(2,1)S(1)}, u32[]{:S(2)}, u32[]{:S(2)}) collective-permute-start(bf16[176,512]{1,0:T(8,128)(2,1)S(1)} %get-tuple-element.18), channel_id=1, source_target_pairs={{0,2},{2,0},{4,6},{6,4},{8,10},{10,8},{12,14},{14,12},{16,18},{18,... | collective-permute-start | bytes 540680 | tf_op jit(solution)/shard_map/ppermute | solution.py:27
  10.3 1.3 %collective-permute-start.4 = (bf16[64,384]{1,0:T(8,128)(2,1)S(1)}, bf16[64,384]{1,0:T(8,128)(2,1)S(1)}, u32[]{:S(2)}, u32[]{:S(2)}) collective-permute-start(bf16[64,384]{1,0:T(8,128)(2,1)S(1)} %get-tuple-element.20), channel_id=1, source_target_pairs={{2,4},{4,2},{6,8},{8,6},{10,12},{12,10},{14,16},{16,14},{18,20},{2... | collective-permute-start | bytes 147464 | tf_op jit(solution)/shard_map/ppermute | solution.py:27
  15.0 14.1 %collective-permute-start.5 = (bf16[192,384]{1,0:T(8,128)(2,1)S(1)}, bf16[192,384]{1,0:T(8,128)(2,1)S(1)}, u32[]{:S(2)}, u32[]{:S(2)}) collective-permute-start(bf16[192,384]{1,0:T(8,128)(2,1)S(1)} %get-tuple-element.23), channel_id=1, source_target_pairs={{0,2},{2,0},{4,6},{6,4},{8,10},{10,8},{12,14},{14,12},{16,18},{18,... | collective-permute-start | bytes 442376 | tf_op jit(solution)/shard_map/ppermute | solution.py:27
  18.8 3.4 %copy-start = (bf16[1,1,2048,2048]{3,2,1,0:T(8,128)(2,1)S(1)}, bf16[1,1,2048,2048]{3,2,1,0:T(8,128)(2,1)}, u32[]{:S(2)}) copy-start(bf16[1,1,2048,2048]{3,2,1,0:T(8,128)(2,1)} %param.10) | copy-start | bytes 25165828
  22.2 3.4 %copy-start.1 = (bf16[1,1,2048,2048]{3,2,1,0:T(8,128)(2,1)S(1)}, bf16[1,1,2048,2048]{3,2,1,0:T(8,128)(2,1)}, u32[]{:S(2)}) copy-start(bf16[1,1,2048,2048]{3,2,1,0:T(8,128)(2,1)} %param.10) | copy-start | bytes 25165828
  25.1 40.1 %collective-permute-start.11 = (bf16[512,384]{1,0:T(8,128)(2,1)S(1)}, bf16[512,384]{1,0:T(8,128)(2,1)S(1)}, u32[]{:S(2)}, u32[]{:S(2)}) collective-permute-start(bf16[512,384]{1,0:T(8,128)(2,1)S(1)} %shard_map.97.refs_0_), channel_id=1, source_target_pairs={{0,2},{2,0},{4,6},{6,4},{8,10},{10,8},{12,14},{14,12},{16,18},{18,... | collective-permute-start | bytes 1179656 | tf_op jit(solution)/shard_map/ppermute | solution.py:27
  28.4 36.8 %collective-permute-start.12 = (bf16[512,384]{1,0:T(8,128)(2,1)S(1)}, bf16[512,384]{1,0:T(8,128)(2,1)S(1)}, u32[]{:S(2)}, u32[]{:S(2)}) collective-permute-start(bf16[512,384]{1,0:T(8,128)(2,1)S(1)} %shard_map.98.refs_1_), channel_id=1, source_target_pairs={{2,4},{4,2},{6,8},{8,6},{10,12},{12,10},{14,16},{16,14},{18,20},{2... | collective-permute-start | bytes 1179656 | tf_op jit(solution)/shard_map/ppermute | solution.py:27
  29.8 7.9 %collective-permute-start.8 = (bf16[64,384]{1,0:T(8,128)(2,1)S(1)}, bf16[64,384]{1,0:T(8,128)(2,1)S(1)}, u32[]{:S(2)}, u32[]{:S(2)}) collective-permute-start(bf16[64,384]{1,0:T(8,128)(2,1)S(1)} %get-tuple-element.30), channel_id=1, source_target_pairs={{0,4},{2,6},{4,0},{6,2},{8,12},{10,14},{12,8},{14,10},{16,20},{18,... | collective-permute-start | bytes 147464 | tf_op jit(solution)/shard_map/ppermute | solution.py:414
  36.9 28.3 %collective-permute-start.13 = (bf16[512,384]{1,0:T(8,128)(2,1)S(1)}, bf16[512,384]{1,0:T(8,128)(2,1)S(1)}, u32[]{:S(2)}, u32[]{:S(2)}) collective-permute-start(bf16[512,384]{1,0:T(8,128)(2,1)S(1)} %shard_map.99.refs_2_), channel_id=1, source_target_pairs={{0,1},{1,0},{2,3},{3,2},{4,5},{5,4},{6,7},{7,6},{8,9},{9,8},{10,11... | collective-permute-start | bytes 1179656 | tf_op jit(solution)/shard_map/ppermute | solution.py:27
  37.0 13.3 %collective-permute-start.6 = (bf16[192,384]{1,0:T(8,128)(2,1)S(1)}, bf16[192,384]{1,0:T(8,128)(2,1)S(1)}, u32[]{:S(2)}, u32[]{:S(2)}) collective-permute-start(bf16[192,384]{1,0:T(8,128)(2,1)S(1)} %get-tuple-element.26.refs_4_), channel_id=1, source_target_pairs={{2,4},{4,2},{6,8},{8,6},{10,12},{12,10},{14,16},{16,14},{18,20},{2... | collective-permute-start | bytes 442376 | tf_op jit(solution)/shard_map/ppermute | solution.py:27
  37.7 11.9 %collective-permute-start.9 = (bf16[64,384]{1,0:T(8,128)(2,1)S(1)}, bf16[64,384]{1,0:T(8,128)(2,1)S(1)}, u32[]{:S(2)}, u32[]{:S(2)}) collective-permute-start(bf16[64,384]{1,0:T(8,128)(2,1)S(1)} %fusion.11), channel_id=1, source_target_pairs={{0,8},{2,10},{4,12},{6,14},{8,0},{10,2},{12,4},{14,6},{16,24},{18,... | collective-permute-start | bytes 147464 | tf_op jit(solution)/shard_map/ppermute | solution.py:414
  49.6 6.1 %collective-permute-start.2 = (bf16[112,512]{1,0:T(8,128)(2,1)S(1)}, bf16[112,512]{1,0:T(8,128)(2,1)S(1)}, u32[]{:S(2)}, u32[]{:S(2)}) collective-permute-start(bf16[112,512]{1,0:T(8,128)(2,1)S(1)} %get-tuple-element.19), channel_id=1, source_target_pairs={{2,4},{4,2},{6,8},{8,6},{10,12},{12,10},{14,16},{16,14},{18,20},{2... | collective-permute-start | bytes 344072 | tf_op jit(solution)/shard_map/ppermute | solution.py:27
  50.3 13.8 %collective-permute-start.7 = (bf16[192,384]{1,0:T(8,128)(2,1)S(1)}, bf16[192,384]{1,0:T(8,128)(2,1)S(1)}, u32[]{:S(2)}, u32[]{:S(2)}) collective-permute-start(bf16[192,384]{1,0:T(8,128)(2,1)S(1)} %collective-permute-done.6.refs_5_), channel_id=1, source_target_pairs={{0,2},{2,0},{4,6},{6,4},{8,10},{10,8},{12,14},{14,12},{16,18},{18,... | collective-permute-start | bytes 442376 | tf_op jit(solution)/shard_map/ppermute | solution.py:27
  55.7 9.5 %collective-permute-start.10 = (bf16[64,384]{1,0:T(8,128)(2,1)S(1)}, bf16[64,384]{1,0:T(8,128)(2,1)S(1)}, u32[]{:S(2)}, u32[]{:S(2)}) collective-permute-start(bf16[64,384]{1,0:T(8,128)(2,1)S(1)} %get-tuple-element.31), channel_id=1, source_target_pairs={{0,16},{2,18},{4,20},{6,22},{8,24},{10,26},{12,28},{14,30},{16,0},... | collective-permute-start | bytes 147464 | tf_op jit(solution)/shard_map/ppermute | solution.py:414
  61.3 2.8 %copy-start.4 = (f32[64,64]{1,0:T(8,128)S(1)}, f32[64,64]{1,0:T(8,128)}, u32[]{:S(2)}) copy-start(f32[64,64]{1,0:T(8,128)} %refs_7_.1) | copy-start | bytes 49156
